TPU v7x, 32 devices: a whole 2x2x4 slice. The times are simulated.
32 devices in a mesh: expert: 4 (over y, x), ffn: 8 (over z, core).
Axes of the slice: x: 2, y: 2, z: 4, core: 2. Of those that a mesh axis runs over, the one named last changes fastest.
Arguments:
- tokens: bfloat16 [1024, 4096], P('expert'), may hold values from -6 to 6
- router_gates: float32 [1024, 2], P('expert'), may hold values from 0.1 to 1
- routes: int32 [1024, 2], P('expert'), may hold values from 0 to 3, all different within a row; in each aligned block of 256 rows (0 to 255, 256 to 511, ...) at most 256 rows name the same one
- gate_proj: bfloat16 [4, 4096, 14336], P('expert', None, 'ffn'), may hold values from -0.09375 to 0.09375
- up_proj: bfloat16 [4, 4096, 14336], P('expert', None, 'ffn'), may hold values from -0.09375 to 0.09375
- down_proj: bfloat16 [4, 14336, 4096], P('expert', 'ffn'), may hold values from -0.0625 to 0.0625
Outputs:
- mixed: bfloat16 [1024, 4096], P('expert', 'ffn')
Inputs may be any that keep to these rules, and one draw needn't show every extreme that they name: `routes`: the 2 experts of a token differ. Among the tokens of one index of the expert axis (aligned blocks of 256 tokens) no expert is chosen by more than 256 tokens, and in some blocks one expert is chosen by exactly 256.
All inputs are finite; a program needn't handle non-finite values.
Results may differ from a plain program's by a relative error of at most 0.017.
Values may be sent and summed in bfloat16 or wider, within the bound.
A program may use at most 128 MiB of HBM per device.

v0:
```python
import functools

import jax
import jax.numpy as jnp
from jax import lax
from jax.experimental import pallas as pl
from jax.experimental.pallas import tpu as pltpu
from jax.sharding import PartitionSpec as P

MESH = pl.DeviceIdType.MESH
VMEM_BYTES = 67043328


def flip(index, mask, size):
    result, bit = 0, 1
    while bit < size:
        digit = (index // bit) % 2
        result = result + bit * ((1 - digit) if mask & bit else digit)
        bit *= 2
    return result


def layer_kernel(
    experts, groups, tile, out_tile,
    tokens_hbm, gates_ref, routes_ref, gate_hbm, up_hbm, down_hbm,
    out_ref,
    gate, up, down, blk, hid, part, pair, returned, *rest,
):
    stages = groups.bit_length() - 2
    stage_in, rest = rest[:stages], rest[stages:]
    (gate_sem, up_sem, down_sem, own_sem, tok_s, tok_r, fwd_s, fwd_r, diag_s, diag_r,
     pair_s, pair_r, stage_s, stage_r, ret_s, ret_r) = rest
    rows, width = blk.shape[1], blk.shape[2]
    hidden = gate.shape[1]
    half, quarter = rows // 2, rows // 4
    eighth = quarter // 2
    cols = width // groups
    count = groups // 2
    tiles, out_tiles = hidden // tile, width // out_tile
    per_tile = out_tile // cols
    e, f = lax.axis_index("expert"), lax.axis_index("ffn")
    core = f % 2
    near = {k: (flip(e, k, experts), f) for k in range(1, experts)}
    mates = [(e, flip(f, 1 << s, groups)) for s in range(stages + 1)]

    barrier = pltpu.get_barrier_semaphore()
    partners = list(near.values()) + mates
    for partner in partners:
        pl.semaphore_signal(barrier, inc=1, device_id=partner, device_id_type=MESH)

    def gate_copy(j):
        s = pl.ds(j * tile, tile)
        return pltpu.make_async_copy(gate_hbm.at[:, s], gate.at[:, s], gate_sem.at[j])

    def up_copy(j):
        s = pl.ds(j * tile, tile)
        return pltpu.make_async_copy(up_hbm.at[:, s], up.at[:, s], up_sem.at[j])

    def down_copy(n):
        s = pl.ds(n * out_tile, out_tile)
        return pltpu.make_async_copy(down_hbm.at[:, s], down.at[:, s], down_sem.at[n])

    own_copy = pltpu.make_async_copy(tokens_hbm, blk.at[0], own_sem)
    own_copy.start()
    for j in range(tiles):
        gate_copy(j).start()
        up_copy(j).start()
    for n in range(out_tiles):
        down_copy(n).start()

    def place(k, h):
        return (1 + h, (k - 1) * half) if k < 3 else (k, h * half)

    def remote(src, dst, ss, rs, device):
        return pltpu.make_async_remote_copy(
            src_ref=src, dst_ref=dst, send_sem=ss, recv_sem=rs, device_id=device, device_id_type=MESH
        )

    def spot(k, h):
        b, row = place(k, h)
        return blk.at[b, pl.ds(pl.multiple_of(row + core * quarter, quarter), quarter)]

    def token_copy(k, h):
        row = pl.multiple_of(h * half + core * quarter, quarter)
        return remote(tokens_hbm.at[pl.ds(row, quarter)], spot(k, h), tok_s.at[k, h], tok_r.at[k, h], near[k])

    def forward_copy(k, h):
        return remote(spot(k, h), spot(k, h), fwd_s.at[k, h], fwd_r.at[k, h], mates[0])

    def diag_copy(i, h):
        source, offset = (2, 0) if i == 0 else (1, eighth)
        b, row = place(source, h)
        src = blk.at[b, pl.ds(pl.multiple_of(row + core * quarter + offset, eighth), eighth)]
        b, row = place(3, h)
        dst = blk.at[b, pl.ds(pl.multiple_of(row + core * quarter + offset, eighth), eighth)]
        return remote(src, dst, diag_s.at[i, h], diag_r.at[i, h], near[1 + i])

    pl.semaphore_wait(barrier, len(partners))
    direct = [k for k in range(1, experts) if k != 3]
    for h in range(2):
        for k in (1, 2):
            token_copy(k, h).start()
    for k in direct[2:]:
        for h in range(2):
            token_copy(k, h).start()

    def pass_on(h):
        for k in (1, 2):
            token_copy(k, h).wait_recv()
            forward_copy(k, h).start()
        for i in range(2):
            diag_copy(i, h).start()

    def prepare(b):
        if b < 3:
            pass_on(b - 1)
        elif b == 3:
            for h in range(2):
                for i in range(2):
                    diag_copy(i, h).wait_recv()
                forward_copy(3, h).start()
        else:
            for h in range(2):
                token_copy(b, h).wait_recv()
                forward_copy(b, h).start()

    def arrive(b):
        pairs = [(1, b - 1), (2, b - 1)] if b < 3 else [(b, 0), (b, 1)]
        for k, h in pairs:
            forward_copy(k, h).wait_recv()

    def pair_copy(b, n):
        return remote(part.at[1, n], pair.at[b, n], pair_s.at[b, n], pair_r.at[b, n], mates[0])

    def kept(stage, m):
        index, low = 0, 1
        for s in range(1, stage + 1):
            index = index + low * ((f // (1 << s)) % 2)
            low *= 2
        return index + low * m

    def stage_copy(stage, b, m):
        low = 1 << (stage - 1)
        digit = (f // (1 << stage)) % 2
        base = kept(stage - 1, 0)
        src = pair.at[b, base + low * (1 - digit) + 2 * low * m]
        return remote(
            src, stage_in[stage - 1].at[b, m],
            stage_s.at[stage - 1, b, m], stage_r.at[stage - 1, b, m], mates[stage],
        )

    def pieces(stage):
        return count >> stage

    def join_pair(b):
        for n in range(count):
            pair_copy(b, n).wait()
            pair[b, n] = (part[0, n].astype(jnp.float32) + pair[b, n].astype(jnp.float32)).astype(pair.dtype)
        for m in range(pieces(1)):
            stage_copy(1, b, m).start()

    def join_stage(stage, b):
        for m in range(pieces(stage)):
            stage_copy(stage, b, m).wait()
            at = kept(stage, m)
            got = stage_in[stage - 1][b, m].astype(jnp.float32)
            pair[b, at] = (pair[b, at].astype(jnp.float32) + got).astype(pair.dtype)
        if stage < stages:
            for m in range(pieces(stage + 1)):
                stage_copy(stage + 1, b, m).start()

    def return_copy(b, j):
        k, h = (j + 1, b - 1) if b < 3 else (b, j)
        src = pair.at[b, f // 2, pl.ds(j * half, half)]
        return remote(
            src, returned.at[k - 1, pl.ds(h * half, half)], ret_s.at[k, h], ret_r.at[k, h], near[k]
        )

    def give_back(b):
        if b > 0:
            for j in range(2):
                return_copy(b, j).start()

    def compute(b, first, hooks):
        for j in range(tiles):
            if first:
                if j == 0:
                    own_copy.wait()
                gate_copy(j).wait()
                up_copy(j).wait()
            s = pl.ds(j * tile, tile)
            gate_act = jnp.dot(blk[b], gate[:, s], preferred_element_type=jnp.float32)
            up_act = jnp.dot(blk[b], up[:, s], preferred_element_type=jnp.float32)
            hid[:, s] = (gate_act / (1.0 + jnp.exp(-gate_act)) * up_act).astype(hid.dtype)
            hooks(("mid", j))
        for n in range(out_tiles):
            if first:
                down_copy(n).wait()
            s = pl.ds(n * out_tile, out_tile)
            acc = jnp.dot(hid[...], down[:, s], preferred_element_type=jnp.float32).astype(part.dtype)
            for i in range(per_tile):
                block = n * per_tile + i
                part[(block + core) % 2, block // 2] = acc[:, i * cols : (i + 1) * cols]
            for m in range(n * per_tile // 2, (n + 1) * per_tile // 2):
                pair_copy(b, m).start()
            hooks(("end", n))

    def first_hooks(at):
        if at == ("end", out_tiles // 2 - 1):
            prepare(1)

    compute(0, True, first_hooks)

    @pl.loop(1, experts)
    def _(step):
        for b in range(1, experts):
            @pl.when(step == b)
            def _():
                arrive(b)

        def hooks(at):
            if at == ("mid", 0):
                join_pair(step - 1)
            if at == ("mid", 1):
                @pl.when(step >= 2)
                def _():
                    join_stage(1, step - 2)
            if at == ("mid", tiles - 1):
                for b in range(1, experts - 1):
                    @pl.when(step == b)
                    def _():
                        prepare(b + 1)

        compute(step, False, hooks)

    join_pair(experts - 1)
    for b in range(experts - 2):
        for stage in range(2, stages + 1):
            join_stage(stage, b)
        give_back(b)
    for b in range(experts - 2, experts):
        join_stage(1, b)
    for b in range(experts - 2, experts):
        for stage in range(2, stages + 1):
            join_stage(stage, b)
        give_back(b)

    for k in range(1, experts):
        for h in range(2):
            if k != 3:
                token_copy(k, h).wait_send()
            forward_copy(k, h).wait_send()
    for i in range(2):
        for h in range(2):
            diag_copy(i, h).wait_send()

    def weight_of(k):
        name = flip(e, k, experts)
        total = jnp.zeros((rows, 1), jnp.float32)
        for t in range(routes_ref.shape[1]):
            total = total + jnp.where(routes_ref[:, t : t + 1] == name, gates_ref[:, t : t + 1], 0.0)
        return total

    result = weight_of(0) * pair[0, f // 2].astype(jnp.float32)
    for b in range(1, experts):
        for j in range(2):
            return_copy(b, j).wait()
    for k in range(1, experts):
        result = result + weight_of(k) * returned[k - 1].astype(jnp.float32)
    out_ref[...] = result.astype(out_ref.dtype)


def per_device(experts, groups, tokens, router_gates, routes, gate_proj, up_proj, down_proj):
    rows, width = tokens.shape
    hidden = gate_proj.shape[2]
    cols = width // groups
    count = groups // 2
    stages = groups.bit_length() - 2
    tile = 256 if hidden % 256 == 0 else 128
    out_tile = 1024
    bf16 = jnp.bfloat16
    dma = pltpu.SemaphoreType.DMA
    vmem = pl.BlockSpec(memory_space=pltpu.VMEM)
    hbm = pl.BlockSpec(memory_space=pl.ANY)
    scratch = [
        pltpu.VMEM((width, hidden), bf16),
        pltpu.VMEM((width, hidden), bf16),
        pltpu.VMEM((hidden, width), bf16),
        pltpu.VMEM((experts, rows, width), bf16),
        pltpu.VMEM((rows, hidden), bf16),
        pltpu.VMEM((2, count, rows, cols), bf16),
        pltpu.VMEM((experts, count, rows, cols), bf16),
        pltpu.VMEM((experts - 1, rows, cols), bf16),
    ]
    scratch += [pltpu.VMEM((experts, count >> s, rows, cols), bf16) for s in range(1, stages + 1)]
    scratch += [
        dma((hidden // tile,)), dma((hidden // tile,)), dma((width // out_tile,)), dma,
        dma((experts, 2)), dma((experts, 2)), dma((experts, 2)), dma((experts, 2)),
        dma((2, 2)), dma((2, 2)),
        dma((experts, count)), dma((experts, count)),
        dma((stages, experts, count // 2)), dma((stages, experts, count // 2)),
        dma((experts, 2)), dma((experts, 2)),
    ]
    return pl.pallas_call(
        functools.partial(layer_kernel, experts, groups, tile, out_tile),
        name="layer",
        out_shape=jax.ShapeDtypeStruct((rows, cols), bf16),
        in_specs=[hbm, vmem, vmem, hbm, hbm, hbm],
        out_specs=vmem,
        scratch_shapes=scratch,
        compiler_params=pltpu.CompilerParams(
            collective_id=0, has_side_effects=True, vmem_limit_bytes=VMEM_BYTES
        ),
    )(tokens, router_gates, routes, gate_proj[0], up_proj[0], down_proj[0])


def solution(mesh):
    in_specs = (
        P("expert", None),
        P("expert", None),
        P("expert", None),
        P("expert", None, "ffn"),
        P("expert", None, "ffn"),
        P("expert", "ffn", None),
    )
    body = functools.partial(per_device, mesh.shape["expert"], mesh.shape["ffn"])
    return jax.shard_map(
        body, mesh=mesh, in_specs=in_specs, out_specs=P("expert", "ffn"), check_vma=False
    )
```

profile of v0, /device:TPU:0, one launch (start us, length us, event | category | flops | bytes accessed | tf_op | source)
XLA Modules:
  0.0 125.6 jit_solution(12535184856247935746)
XLA Ops:
  0.0 1.5 %copy.7.gates_ref = f32[256,2]{1,0:T(8,128)} copy(f32[256,2]{0,1:T(2,128)} %param.7) | data formatting | bytes 4096 | tf_op args[1]
  1.5 1.5 %copy.8.routes_ref = s32[256,2]{1,0:T(8,128)} copy(s32[256,2]{0,1:T(2,128)} %param.8) | data formatting | bytes 4096 | tf_op args[2]
  3.0 120.9 %layer.1 = bf16[256,512]{1,0:T(8,128)(2,1)} custom-call(bf16[256,4096]{1,0:T(8,128)(2,1)} %tokens_hbm.1, f32[256,2]{1,0:T(8,128)} %copy.7.gates_ref, s32[256,2]{1,0:T(8,128)} %copy.8.routes_ref, bf16[4096,1792]{1,0:T(8,128)(2,1)} %bitcast.3, bf16[4096,1792]{1,0:T(8,128)(2,1)} %bitcast.4, bf16[1792,4096]{1,0:T(8,128)(2,1)} %bitcast.5), custom_call_target="tpu_custom_call" | custom-call | tf_op jit(solution)/shard_map/layer/pallas_call | solution.py:304
  123.9 1.7 %copy.10 = bf16[256,512]{1,0:T(8,128)(2,1)} copy(bf16[256,512]{1,0:T(8,128)(2,1)} %layer.1) | data formatting | bytes 524288
where the time goes:
time: 126 us
  Pallas kernels  121 us (96%)
  local copies, waits for them, and re-layouts  4.62 us (4%)
    pallas_call x1, Pallas kernels, per_device(): pl.pallas_call(functools.partial(layer_kernel, experts, groups, tile, out...  121 us
    unnamed x3, local copies, waits for them, and re-layouts  4.62 us

commit v1 on v0

v1 whole, which is shorter than its diff:
```python
import functools

import jax
import jax.numpy as jnp
from jax import lax
from jax.experimental import pallas as pl
from jax.experimental.pallas import tpu as pltpu
from jax.sharding import PartitionSpec as P

MESH = pl.DeviceIdType.MESH
VMEM_BYTES = 67043328
AHEAD = 3


def flip(index, mask, size):
    result, bit = 0, 1
    while bit < size:
        digit = (index // bit) % 2
        result = result + bit * ((1 - digit) if mask & bit else digit)
        bit *= 2
    return result


def layer_kernel(
    experts, groups, tile,
    tokens_hbm, gates_ref, routes_ref, gate_hbm, up_hbm, down_hbm,
    out_ref,
    gate, up, down, blk, hid, part, pair, returned, table, their_gates, their_routes, their_table,
    *rest,
):
    stages = groups.bit_length() - 2
    sum_in, far_in, rest = rest[:stages], rest[stages : 2 * stages], rest[2 * stages :]
    (weight_sem, own_sem, tok_s, tok_r, fwd_s, fwd_r, relay_s, relay_r,
     pair_s, pair_r, met_s, met_r, stage_s, stage_r, ret_s, ret_r,
     detour_s, detour_r, route_s, route_r) = rest
    rows, width = blk.shape[1], blk.shape[2]
    hidden = gate.shape[1]
    half, quarter, piece = rows // 2, rows // 4, rows // 8
    cols = width // groups
    count = groups // 2
    tiles, out_tile = hidden // tile, 2 * cols
    last = experts - 1
    e, f = lax.axis_index("expert"), lax.axis_index("ffn")
    core = f % 2
    near = {k: (flip(e, k, experts), f) for k in range(1, experts)}
    mates = [(e, flip(f, 1 << s, groups)) for s in range(stages + 1)]
    far = list(range(3, experts))
    f32 = jnp.float32

    barrier = pltpu.get_barrier_semaphore()
    partners = list(near.values()) + mates
    for partner in partners:
        pl.semaphore_signal(barrier, inc=1, device_id=partner, device_id_type=MESH)

    own_copy = pltpu.make_async_copy(tokens_hbm, blk.at[0], own_sem)

    def columns(t):
        index = 0
        for s in range(1, stages + 1):
            digit = (f // (1 << s)) % 2
            index = index + (1 << (s - 1)) * (digit if (t >> (stages - s)) & 1 else 1 - digit)
        return pl.ds(pl.multiple_of(index * out_tile, out_tile), out_tile)

    def weight_group(i):
        if i < tiles:
            s = pl.ds(i * tile, tile)
            return [
                pltpu.make_async_copy(gate_hbm.at[:, s], gate.at[:, s], weight_sem.at[0, i]),
                pltpu.make_async_copy(up_hbm.at[:, s], up.at[:, s], weight_sem.at[1, i]),
            ]
        s = columns(i - tiles)
        return [pltpu.make_async_copy(down_hbm.at[:, s], down.at[:, s], weight_sem.at[0, i])]

    def start_weights(i):
        if i < tiles + count:
            for copy in weight_group(i):
                copy.start()

    def take_weights(i):
        for copy in weight_group(i):
            copy.wait()
        start_weights(i + AHEAD)

    own_copy.start()
    for i in range(AHEAD):
        start_weights(i)

    def place(k, h):
        return (last if h else 1, (k - 1) * half) if k < 3 else (k - 1, h * half)

    def remote(src, dst, ss, rs, device):
        return pltpu.make_async_remote_copy(
            src_ref=src, dst_ref=dst, send_sem=ss, recv_sem=rs, device_id=device, device_id_type=MESH
        )

    def spot(k, h, i):
        b, row = place(k, h)
        return blk.at[b, pl.ds(pl.multiple_of(row + core * quarter + i * piece, piece), piece)]

    def token_copy(k, h, i):
        row = pl.multiple_of(h * half + core * quarter + i * piece, piece)
        return remote(
            tokens_hbm.at[pl.ds(row, piece)], spot(k, h, i), tok_s.at[k, h, i], tok_r.at[k, h, i], near[k]
        )

    def forward_copy(k, h, i):
        return remote(spot(k, h, i), spot(k, h, i), fwd_s.at[k, h, i], fwd_r.at[k, h, i], mates[0])

    def weight_rows(gates, routes, name):
        total = jnp.zeros((1, rows), f32)
        for t in range(routes.shape[0]):
            total = total + jnp.where(routes[t : t + 1, :] == name, gates[t : t + 1, :], 0.0)
        return jnp.broadcast_to(total, (128, rows)).T

    def route_copies(k):
        return [
            remote(ref, theirs.at[k - 1], route_s.at[i, k - 1], route_r.at[i, k - 1], near[k])
            for i, (ref, theirs) in enumerate([(gates_ref, their_gates), (routes_ref, their_routes)])
        ]

    def relay_copy(i):
        return remote(spot(2 - i, 0, i), spot(3, 0, i), relay_s.at[i], relay_r.at[i], near[1 + i])

    for k in range(experts):
        table[k] = weight_rows(gates_ref[...], routes_ref[...], flip(e, k, experts))
    pl.semaphore_wait(barrier, len(partners))
    for i in range(2):
        for k in (1, 2):
            token_copy(k, 0, i).start()
    for k in (1, 2):
        for copy in route_copies(k):
            copy.start()
    for k in far:
        for h in range(1 if k == 3 else 0, 2):
            for i in range(2):
                token_copy(k, h, i).start()

    def pass_first(i):
        for k in (1, 2):
            token_copy(k, 0, i).wait_recv()
            forward_copy(k, 0, i).start()
        relay_copy(i).start()

    def send_second():
        for i in range(2):
            for k in (1, 2):
                token_copy(k, 1, i).start()

    def pass_second():
        for i in range(2):
            for k in (1, 2):
                token_copy(k, 1, i).wait_recv()
                forward_copy(k, 1, i).start()

    def pass_far(k):
        for h in (1, 0):
            for i in range(2):
                if k == 3 and h == 0:
                    relay_copy(i).wait_recv()
                else:
                    token_copy(k, h, i).wait_recv()
                forward_copy(k, h, i).start()

    def arrive(b):
        if b in (1, last):
            pairs = [(1, b // last), (2, b // last)]
        else:
            pairs = [(b + 1, 0), (b + 1, 1)]
        for k, h in pairs:
            for i in range(2):
                forward_copy(k, h, i).wait_recv()

    def pair_copy(b, n):
        return remote(part.at[1, n], pair.at[b, n], pair_s.at[b, n], pair_r.at[b, n], mates[0])

    def join_pair(b, n):
        pair_copy(b, n).wait()
        pair[b, n] = (part[0, n].astype(f32) + pair[b, n].astype(f32)).astype(pair.dtype)

    def met_copy(k, n):
        b, row = place(k, 1)
        return remote(
            pair.at[b, n, pl.ds(row, half)], met(k, n), met_s.at[k - 1, n], met_r.at[k - 1, n], near[k]
        )

    def hand_over(n):
        join_pair(last, n)
        add_detour(n)
        for k in (1, 2):
            met_copy(k, n).start()

    def weight_of(k, h):
        return table[k, pl.ds(h * half, half), 0:1]

    def learn_routes():
        for k in (1, 2):
            for copy in route_copies(k):
                copy.wait_recv()
            for i, name in enumerate([e, near[3 - k][0]]):
                their_table[k - 1, i] = weight_rows(their_gates[k - 1], their_routes[k - 1], name)[half:]

    def met(k, n):
        return blk.at[0, pl.ds((k - 1) * half, half), pl.ds(n * cols, cols)]

    def detour(k, n):
        return blk.at[0, pl.ds((k - 1) * quarter, quarter), pl.ds(width // 2 + n * cols, cols)]

    def home(k):
        if k < 4:
            return blk.at[0, pl.ds(half, half), pl.ds(width // 2 + (k - 1) * cols, cols)]
        return returned.at[k - 4]

    def detour_copy(k, n):
        src = pair.at[2, n, pl.ds(half + (2 - k) * quarter, quarter)]
        return remote(src, detour(k, n), detour_s.at[k - 1, n], detour_r.at[k - 1, n], near[k])

    def add_detour(n):
        for k in (1, 2):
            detour_copy(k, n).wait_recv()
        for k in (1, 2):
            for i in range(2):
                here = pair.at[last, n, pl.ds((k - 1) * half + i * quarter, quarter)]
                s = pl.ds(i * quarter, quarter)
                total = their_table[k - 1, 0, s, 0:1] * here[...].astype(f32)
                if i == k - 1:
                    total = total + their_table[k - 1, 1, s, 0:1] * detour(3 - k, n)[...].astype(f32)
                here[...] = total.astype(pair.dtype)

    def first_of(stage):
        return count - (count >> stage)

    def view(task, n):
        if task < 2:
            return pair.at[0, n, pl.ds(task * half, half)]
        if task == 3:
            return pair.at[2, n, pl.ds(0, half)]
        return pair.at[task - 1, n]

    def inbox(stage, task, m):
        if task < 2:
            return sum_in[stage - 1].at[task, m]
        if task == 3:
            return far_in[stage - 1].at[1, m, pl.ds(0, half)]
        return far_in[stage - 1].at[task - 2, m]

    def stage_copy(stage, task, m):
        return remote(
            view(task, first_of(stage - 1) + m), inbox(stage, task, m),
            stage_s.at[stage - 1, task, m], stage_r.at[stage - 1, task, m], mates[stage],
        )

    def send_stage(stage, task):
        for m in range(count >> stage):
            stage_copy(stage, task, m).start()

    def join_piece(stage, task, m):
        stage_copy(stage, task, m).wait()
        here = view(task, first_of(stage) + m)
        total = here[...].astype(f32) + inbox(stage, task, m)[...].astype(f32)
        here[...] = total.astype(pair.dtype)

    def join_stage(stage, task):
        for m in range(count >> stage):
            join_piece(stage, task, m)
        if stage < stages:
            send_stage(stage + 1, task)

    def meet(n):
        here = view(1, n)
        total = weight_of(0, 1) * here[...].astype(f32)
        for k in (1, 2):
            met_copy(k, n).wait_recv()
            total = total + met(k, n)[...].astype(f32)
        here[...] = total.astype(pair.dtype)
        for stage in range(1, stages + 1):
            if n < first_of(stage):
                stage_copy(stage, 1, n - first_of(stage - 1)).start()
                break
            join_piece(stage, 1, n - first_of(stage))

    def return_copies(b):
        done = pair.at[b, count - 1]
        if b == 2:
            return [remote(done.at[pl.ds(0, half)], home(3), ret_s.at[b], ret_r.at[b], near[3])]
        if b > 2:
            return [remote(done, home(b + 1), ret_s.at[b], ret_r.at[b], near[b + 1])]
        return [
            remote(
                done.at[pl.ds((k - 1) * half, half)], home(k),
                ret_s.at[k - 1], ret_r.at[k - 1], near[k],
            )
            for k in (1, 2)
        ]

    def finish(b):
        for stage in range(2, stages + 1):
            join_stage(stage, b + 1)
        for copy in return_copies(b):
            copy.start()

    def compute(b, first, hooks):
        for j in range(tiles):
            if first:
                if j == 0:
                    own_copy.wait()
                take_weights(j)
            s = pl.ds(j * tile, tile)
            gate_act = jnp.dot(blk[b], gate[:, s], preferred_element_type=f32)
            up_act = jnp.dot(blk[b], up[:, s], preferred_element_type=f32)
            hid[:, s] = (gate_act / (1.0 + jnp.exp(-gate_act)) * up_act).astype(hid.dtype)
            hooks("mid", j)
        for t in range(count):
            if first:
                take_weights(tiles + t)
            acc = jnp.dot(hid[...], down[:, columns(t)], preferred_element_type=f32).astype(part.dtype)
            for i in range(2):
                part[(core + i) % 2, t] = acc[:, i * cols : (i + 1) * cols]
            pair_copy(b, t).start()
            hooks("end", t)

    def first_hooks(phase, at):
        if phase == "end" and at < 2:
            pass_first(at)
        if (phase, at) == ("end", 1):
            send_second()

    def actions(step, phase, at):
        todo = []
        if (phase, at) == ("mid", 0):
            if step > 2:
                todo += [functools.partial(join_stage, 1, step - 1)]
            todo += [functools.partial(join_pair, step - 1, n) for n in range(count)]
            if step == 3:
                todo += [lambda k=k, n=n: detour_copy(k, n).start() for n in range(count) for k in (1, 2)]
            todo += [functools.partial(send_stage, 1, step if step > 1 else 0)]
        if (phase, at) == ("mid", 2) and step == 2:
            todo += [learn_routes]
        if (phase, at) == ("mid", 1) and step == 2:
            todo += [functools.partial(join_stage, stage, 0) for stage in range(2, stages + 1)]
        if (phase, at) == ("end", 0):
            if step == 1:
                todo += [functools.partial(join_stage, 1, 0)]
            if step == last - 1:
                todo += [pass_second]
        if (phase, at) == ("end", count - 2) and step < last - 1:
            todo += [functools.partial(pass_far, step + 2)]
        if (phase, at) == ("end", count - 1) and step > 2:
            todo += [functools.partial(finish, step - 2)]
        if step == last and phase == "end" and at > 0:
            todo += [functools.partial(hand_over, at - 1)]
        return todo

    compute(0, True, first_hooks)

    @pl.loop(1, experts)
    def _(step):
        for b in range(1, experts):
            @pl.when(step == b)
            def _():
                arrive(b)

        def hooks(phase, at):
            for b in range(1, experts):
                todo = actions(b, phase, at)
                if todo:
                    @pl.when(step == b)
                    def _():
                        for action in todo:
                            action()

        compute(step, False, hooks)

    hand_over(count - 1)
    join_stage(1, last)
    for n in range(count // 2):
        meet(n)
    finish(last - 1)
    for n in range(count // 2, count):
        meet(n)

    for k in range(1, experts):
        for h in range(2):
            for i in range(2):
                if (k, h) != (3, 0):
                    token_copy(k, h, i).wait_send()
                forward_copy(k, h, i).wait_send()
    for i in range(2):
        relay_copy(i).wait_send()
    for k in (1, 2):
        for copy in route_copies(k):
            copy.wait_send()
        for n in range(count):
            detour_copy(k, n).wait_send()
            met_copy(k, n).wait_send()
    for b in range(1, last):
        for copy in return_copies(b):
            copy.wait()
    for h in range(2):
        s = pl.ds(h * half, half)
        result = view(h, count - 1)[...].astype(f32)
        if h == 0:
            result = weight_of(0, 0) * result
        for k in range(4 if h else 1, experts):
            back = home(k)[...] if k < 4 else returned[k - 4, s]
            result = result + weight_of(k, h) * back.astype(f32)
        out_ref[s] = result.astype(out_ref.dtype)


def per_device(experts, groups, tokens, router_gates, routes, gate_proj, up_proj, down_proj):
    rows, width = tokens.shape
    hidden = gate_proj.shape[2]
    cols = width // groups
    count = groups // 2
    stages = groups.bit_length() - 2
    tile = 256 if hidden % 256 == 0 else 128
    bf16 = jnp.bfloat16
    dma = pltpu.SemaphoreType.DMA
    vmem = pl.BlockSpec(memory_space=pltpu.VMEM)
    hbm = pl.BlockSpec(memory_space=pl.ANY)
    half = rows // 2
    steps = hidden // tile + count
    far = experts - 2
    scratch = [
        pltpu.VMEM((width, hidden), bf16),
        pltpu.VMEM((width, hidden), bf16),
        pltpu.VMEM((hidden, width), bf16),
        pltpu.VMEM((experts, rows, width), bf16),
        pltpu.VMEM((rows, hidden), bf16),
        pltpu.VMEM((2, count, rows, cols), bf16),
        pltpu.VMEM((experts, count, rows, cols), bf16),
        pltpu.VMEM((max(experts - 4, 1), rows if experts > 4 else 16, cols), bf16),
        pltpu.VMEM((experts, rows, 128), jnp.float32),
        pltpu.VMEM((2,) + router_gates.shape[::-1], router_gates.dtype),
        pltpu.VMEM((2,) + routes.shape[::-1], routes.dtype),
        pltpu.VMEM((2, 2, half, 128), jnp.float32),
    ]
    scratch += [pltpu.VMEM((2, count >> s, half, cols), bf16) for s in range(1, stages + 1)]
    scratch += [pltpu.VMEM((far, count >> s, rows, cols), bf16) for s in range(1, stages + 1)]
    scratch += [dma((2, steps)), dma]
    scratch += [dma((experts, 2, 2))] * 4 + [dma((2,))] * 2
    scratch += [dma((experts, count))] * 2 + [dma((2, count))] * 2
    scratch += [dma((stages, 2 + far, count // 2))] * 2 + [dma((experts - 1,))] * 2
    scratch += [dma((2, count))] * 2 + [dma((2, 2))] * 2
    return pl.pallas_call(
        functools.partial(layer_kernel, experts, groups, tile),
        name="layer",
        out_shape=jax.ShapeDtypeStruct((rows, cols), bf16),
        in_specs=[hbm, vmem, vmem, hbm, hbm, hbm],
        out_specs=vmem,
        scratch_shapes=scratch,
        compiler_params=pltpu.CompilerParams(
            collective_id=0, has_side_effects=True, vmem_limit_bytes=VMEM_BYTES
        ),
    )(tokens, router_gates.T, routes.T, gate_proj[0], up_proj[0], down_proj[0])


def solution(mesh):
    in_specs = (
        P("expert", None),
        P("expert", None),
        P("expert", None),
        P("expert", None, "ffn"),
        P("expert", None, "ffn"),
        P("expert", "ffn", None),
    )
    body = functools.partial(per_device, mesh.shape["expert"], mesh.shape["ffn"])
    return jax.shard_map(
        body, mesh=mesh, in_specs=in_specs, out_specs=P("expert", "ffn"), check_vma=False
    )
```

time: 126 us -> 89.2 us (0.71)
  Pallas kernels: 121 us -> 87.4 us
  local copies, waits for them, and re-layouts: 4.62 us -> 1.67 us
    pallas_call x1, Pallas kernels: 121 us -> 87.4 us  [per_device(): pl.pallas_call(functools.partial(layer_kernel, experts, groups, tile), na...]
    unnamed x3 -> x1, local copies, waits for them, and re-layouts: 4.62 us -> 1.67 us
where the time goes in v1:
time: 89.2 us; the launch traced here: 89.1 us
  Pallas kernels  87.4 us (98%)
  local copies, waits for them, and re-layouts  1.67 us (2%)
    pallas_call x1, Pallas kernels, per_device(): pl.pallas_call(functools.partial(layer_kernel, experts, groups, tile), na...  87.4 us

profile of v1, /device:TPU:0, one launch (start us, length us, event | category | flops | bytes accessed | tf_op | source)
XLA Modules:
  0.0 89.1 jit_solution(14760415322941048187)
XLA Ops:
  0.0 87.4 %layer.1 = bf16[256,512]{1,0:T(8,128)(2,1)} custom-call(bf16[256,4096]{1,0:T(8,128)(2,1)} %tokens_hbm.1, f32[2,256]{1,0:T(2,128)} %bitcast.8, s32[2,256]{1,0:T(2,128)} %bitcast.9, bf16[4096,1792]{1,0:T(8,128)(2,1)} %bitcast.5, bf16[4096,1792]{1,0:T(8,128)(2,1)} %bitcast.6, bf16[1792,4096]{1,0:T(8,128)(2,1)} %bitcast.7), custom_call_target="tpu_custom_call" | custom-call | tf_op jit(solution)/shard_map/layer/pallas_call | solution.py:444
  87.4 1.7 %copy.8 = bf16[256,512]{1,0:T(8,128)(2,1)} copy(bf16[256,512]{1,0:T(8,128)(2,1)} %layer.1) | data formatting | bytes 524288

commit v2 on v1

--- a/solution.py
+++ b/solution.py
@@ -46,6 +46,7 @@
     mates = [(e, flip(f, 1 << s, groups)) for s in range(stages + 1)]
     far = list(range(3, experts))
     f32 = jnp.float32
+    half_of_pair = (f // 2) % 2
 
     barrier = pltpu.get_barrier_semaphore()
     partners = list(near.values()) + mates
@@ -93,12 +94,20 @@
             src_ref=src, dst_ref=dst, send_sem=ss, recv_sem=rs, device_id=device, device_id_type=MESH
         )
 
+    def which(k, h, i):
+        if (k, h) == (3, 1):
+            return 1 - half_of_pair if i else half_of_pair
+        return i
+
     def spot(k, h, i):
         b, row = place(k, h)
-        return blk.at[b, pl.ds(pl.multiple_of(row + core * quarter + i * piece, piece), piece)]
+        return blk.at[b, pl.ds(pl.multiple_of(row + core * quarter + which(k, h, i) * piece, piece), piece)]
 
     def token_copy(k, h, i):
-        row = pl.multiple_of(h * half + core * quarter + i * piece, piece)
+        if (k, h, i) == (3, 1, 1):
+            here = spot(3, 1, 0)
+            return remote(here, here, tok_s.at[k, h, i], tok_r.at[k, h, i], mates[1])
+        row = pl.multiple_of(h * half + core * quarter + which(k, h, i) * piece, piece)
         return remote(
             tokens_hbm.at[pl.ds(row, piece)], spot(k, h, i), tok_s.at[k, h, i], tok_r.at[k, h, i], near[k]
         )
@@ -133,13 +142,25 @@
     for k in far:
         for h in range(1 if k == 3 else 0, 2):
             for i in range(2):
-                token_copy(k, h, i).start()
+                if (k, h, i) != (3, 1, 1):
+                    token_copy(k, h, i).start()
+
+    def share():
+        token_copy(3, 1, 0).wait_recv()
+        forward_copy(3, 1, 0).start()
+        token_copy(3, 1, 1).start()
 
     def pass_first(i):
         for k in (1, 2):
             token_copy(k, 0, i).wait_recv()
             forward_copy(k, 0, i).start()
         relay_copy(i).start()
+
+    def free_first():
+        for i in range(2):
+            relay_copy(i).wait_send()
+            for k in (1, 2):
+                forward_copy(k, 0, i).wait_send()
 
     def send_second():
         for i in range(2):
@@ -155,6 +176,8 @@
     def pass_far(k):
         for h in (1, 0):
             for i in range(2):
+                if (k, h, i) == (3, 1, 0):
+                    continue
                 if k == 3 and h == 0:
                     relay_copy(i).wait_recv()
                 else:
@@ -177,17 +200,18 @@
         pair_copy(b, n).wait()
         pair[b, n] = (part[0, n].astype(f32) + pair[b, n].astype(f32)).astype(pair.dtype)
 
-    def met_copy(k, n):
-        b, row = place(k, 1)
+    def met_copy(k, h, n):
+        b, row = place(k, h)
         return remote(
-            pair.at[b, n, pl.ds(row, half)], met(k, n), met_s.at[k - 1, n], met_r.at[k - 1, n], near[k]
+            pair.at[b, n, pl.ds(row, half)], met(k, h, n),
+            met_s.at[k - 1, h, n], met_r.at[k - 1, h, n], near[k],
         )
 
     def hand_over(n):
         join_pair(last, n)
         add_detour(n)
         for k in (1, 2):
-            met_copy(k, n).start()
+            met_copy(k, 1, n).start()
 
     def weight_of(k, h):
         return table[k, pl.ds(h * half, half), 0:1]
@@ -199,15 +223,15 @@
             for i, name in enumerate([e, near[3 - k][0]]):
                 their_table[k - 1, i] = weight_rows(their_gates[k - 1], their_routes[k - 1], name)[half:]
 
-    def met(k, n):
-        return blk.at[0, pl.ds((k - 1) * half, half), pl.ds(n * cols, cols)]
+    def met(k, h, n):
+        return blk.at[h, pl.ds((k - 1) * half, half), pl.ds(n * cols, cols)]
 
     def detour(k, n):
         return blk.at[0, pl.ds((k - 1) * quarter, quarter), pl.ds(width // 2 + n * cols, cols)]
 
     def home(k):
         if k < 4:
-            return blk.at[0, pl.ds(half, half), pl.ds(width // 2 + (k - 1) * cols, cols)]
+            return blk.at[0, pl.ds(half, half), pl.ds(width // 2, cols)]
         return returned.at[k - 4]
 
     def detour_copy(k, n):
@@ -265,13 +289,18 @@
         if stage < stages:
             send_stage(stage + 1, task)
 
-    def meet(n):
-        here = view(1, n)
-        total = weight_of(0, 1) * here[...].astype(f32)
-        for k in (1, 2):
-            met_copy(k, n).wait_recv()
-            total = total + met(k, n)[...].astype(f32)
+    def meet(h, n):
+        here = view(h, n)
+        total = weight_of(0, h) * here[...].astype(f32)
+        for k in (1, 2):
+            met_copy(k, h, n).wait_recv()
+            got = met(k, h, n)[...].astype(f32)
+            total = total + (got if h else weight_of(k, h) * got)
         here[...] = total.astype(pair.dtype)
+        if n < first_of(1):
+            stage_copy(1, h, n).start()
+
+    def settle(n):
         for stage in range(1, stages + 1):
             if n < first_of(stage):
                 stage_copy(stage, 1, n - first_of(stage - 1)).start()
@@ -282,15 +311,7 @@
         done = pair.at[b, count - 1]
         if b == 2:
             return [remote(done.at[pl.ds(0, half)], home(3), ret_s.at[b], ret_r.at[b], near[3])]
-        if b > 2:
-            return [remote(done, home(b + 1), ret_s.at[b], ret_r.at[b], near[b + 1])]
-        return [
-            remote(
-                done.at[pl.ds((k - 1) * half, half)], home(k),
-                ret_s.at[k - 1], ret_r.at[k - 1], near[k],
-            )
-            for k in (1, 2)
-        ]
+        return [remote(done, home(b + 1), ret_s.at[b], ret_r.at[b], near[b + 1])]
 
     def finish(b):
         for stage in range(2, stages + 1):
@@ -327,27 +348,38 @@
     def actions(step, phase, at):
         todo = []
         if (phase, at) == ("mid", 0):
-            if step > 2:
+            if step == 1:
+                todo += [share]
+            if step == 3:
+                todo += [functools.partial(meet, 0, n) for n in range(count // 2, count)]
+            if step > 3:
                 todo += [functools.partial(join_stage, 1, step - 1)]
             todo += [functools.partial(join_pair, step - 1, n) for n in range(count)]
+            if step == 2:
+                todo += [free_first]
+                todo += [lambda k=k, n=n: met_copy(k, 0, n).start() for n in range(count) for k in (1, 2)]
             if step == 3:
                 todo += [lambda k=k, n=n: detour_copy(k, n).start() for n in range(count) for k in (1, 2)]
-            todo += [functools.partial(send_stage, 1, step if step > 1 else 0)]
+            if step > 2:
+                todo += [functools.partial(send_stage, 1, step)]
+        if (phase, at) == ("end", 1) and step == 2:
+            todo += [functools.partial(meet, 0, n) for n in range(count // 2)]
+        if (phase, at) == ("mid", 2) and step == 3:
+            todo += [functools.partial(join_stage, 1, 0)]
         if (phase, at) == ("mid", 2) and step == 2:
             todo += [learn_routes]
-        if (phase, at) == ("mid", 1) and step == 2:
-            todo += [functools.partial(join_stage, stage, 0) for stage in range(2, stages + 1)]
         if (phase, at) == ("end", 0):
-            if step == 1:
-                todo += [functools.partial(join_stage, 1, 0)]
             if step == last - 1:
                 todo += [pass_second]
-        if (phase, at) == ("end", count - 2) and step < last - 1:
-            todo += [functools.partial(pass_far, step + 2)]
-        if (phase, at) == ("end", count - 1) and step > 2:
-            todo += [functools.partial(finish, step - 2)]
+            if step < last - 1:
+                todo += [functools.partial(pass_far, step + 2)]
+        if (phase, at) == ("end", count - 1):
+            if 3 < step < last:
+                todo += [functools.partial(finish, step - 2)]
         if step == last and phase == "end" and at > 0:
             todo += [functools.partial(hand_over, at - 1)]
+            if at == count - 2:
+                todo += [functools.partial(join_stage, 1, last)]
         return todo
 
     compute(0, True, first_hooks)
@@ -371,36 +403,39 @@
         compute(step, False, hooks)
 
     hand_over(count - 1)
-    join_stage(1, last)
-    for n in range(count // 2):
-        meet(n)
+    if last > 3:
+        finish(last - 2)
+    for n in range(count - 1):
+        meet(1, n)
+        if n >= first_of(1):
+            settle(n)
+    for stage in range(2, stages + 1):
+        join_stage(stage, 0)
     finish(last - 1)
-    for n in range(count // 2, count):
-        meet(n)
+    meet(1, count - 1)
+    settle(count - 1)
 
     for k in range(1, experts):
         for h in range(2):
             for i in range(2):
                 if (k, h) != (3, 0):
                     token_copy(k, h, i).wait_send()
-                forward_copy(k, h, i).wait_send()
-    for i in range(2):
-        relay_copy(i).wait_send()
+                if k > 2 or h:
+                    forward_copy(k, h, i).wait_send()
     for k in (1, 2):
         for copy in route_copies(k):
             copy.wait_send()
         for n in range(count):
             detour_copy(k, n).wait_send()
-            met_copy(k, n).wait_send()
-    for b in range(1, last):
+            for h in range(2):
+                met_copy(k, h, n).wait_send()
+    for b in range(2, last):
         for copy in return_copies(b):
             copy.wait()
     for h in range(2):
         s = pl.ds(h * half, half)
         result = view(h, count - 1)[...].astype(f32)
-        if h == 0:
-            result = weight_of(0, 0) * result
-        for k in range(4 if h else 1, experts):
+        for k in range(4 if h else 3, experts):
             back = home(k)[...] if k < 4 else returned[k - 4, s]
             result = result + weight_of(k, h) * back.astype(f32)
         out_ref[s] = result.astype(out_ref.dtype)
@@ -438,7 +473,7 @@
     scratch += [pltpu.VMEM((far, count >> s, rows, cols), bf16) for s in range(1, stages + 1)]
     scratch += [dma((2, steps)), dma]
     scratch += [dma((experts, 2, 2))] * 4 + [dma((2,))] * 2
-    scratch += [dma((experts, count))] * 2 + [dma((2, count))] * 2
+    scratch += [dma((experts, count))] * 2 + [dma((2, 2, count))] * 2
     scratch += [dma((stages, 2 + far, count // 2))] * 2 + [dma((experts - 1,))] * 2
     scratch += [dma((2, count))] * 2 + [dma((2, 2))] * 2
     return pl.pallas_call(

time: 89.2 us -> 86.7 us (0.972)
  Pallas kernels: 87.4 us -> 84.8 us
    pallas_call x1, Pallas kernels: 87.4 us -> 84.8 us  [per_device(): pl.pallas_call(functools.partial(layer_kernel, experts, groups, tile), na...]
where the time goes in v2:
time: 86.7 us; the launch traced here: 86.5 us
  Pallas kernels  84.8 us (98%)
  local copies, waits for them, and re-layouts  1.67 us (2%)
    pallas_call x1, Pallas kernels, per_device(): pl.pallas_call(functools.partial(layer_kernel, experts, groups, tile), na...  84.8 us

profile of v2, /device:TPU:0, one launch (start us, length us, event | category | flops | bytes accessed | tf_op | source)
XLA Modules:
  0.0 86.5 jit_solution(13105139732849063812)
XLA Ops:
  0.0 84.8 %layer.1 = bf16[256,512]{1,0:T(8,128)(2,1)} custom-call(bf16[256,4096]{1,0:T(8,128)(2,1)} %tokens_hbm.1, f32[2,256]{1,0:T(2,128)} %bitcast.8, s32[2,256]{1,0:T(2,128)} %bitcast.9, bf16[4096,1792]{1,0:T(8,128)(2,1)} %bitcast.5, bf16[4096,1792]{1,0:T(8,128)(2,1)} %bitcast.6, bf16[1792,4096]{1,0:T(8,128)(2,1)} %bitcast.7), custom_call_target="tpu_custom_call" | custom-call | tf_op jit(solution)/shard_map/layer/pallas_call | solution.py:479
  84.8 1.7 %copy.8 = bf16[256,512]{1,0:T(8,128)(2,1)} copy(bf16[256,512]{1,0:T(8,128)(2,1)} %layer.1) | data formatting | bytes 524288
